TPU v7x, 32 devices: a whole 2x2x4 slice. The times are simulated.
32 devices in a mesh: groups: 2 (over x), expert: 16 (over z, y, core).
Axes of the slice: x: 2, y: 2, z: 4, core: 2. Of those that a mesh axis runs over, the one named last changes fastest.
Arguments:
- queries: bfloat16 [256, 4096], P(('groups', 'expert')), parts along dimension 0, may hold values from -150 to 150
- key_cache: bfloat16 [256, 64, 512], P(('groups', 'expert')), parts along dimension 0, may hold values from -7 to 7
- value_cache: bfloat16 [256, 64, 512], P(('groups', 'expert')), parts along dimension 0, may hold values from -6 to 6
- new_key: bfloat16 [256, 512], P(('groups', 'expert')), parts along dimension 0, may hold values from -6 to 6
- new_value: bfloat16 [256, 512], P(('groups', 'expert')), parts along dimension 0, may hold values from -6 to 6
- cache_lengths: int32 [256], P(('groups', 'expert')), parts along dimension 0, may hold values from 2 to 64, as said below
- hidden_in: bfloat16 [2048, 2048], P(('groups', 'expert')), parts along dimension 0, may hold values from -6 to 6
- norm_gain: bfloat16 [2048], replicated, may hold values from 0.5 to 1.5
- router_weight: bfloat16 [2048, 16], replicated, may hold values from -0.125 to 0.125
- expert_ids: int32 [2048, 8], P(('groups', 'expert')), parts along dimension 0, may hold values from 0 to 15, all different within a row; in each aligned block of 64 rows (0 to 63, 64 to 127, ...) at most 64 rows name the same one
- gate_train: bfloat16 [16, 2048, 768], P(None, 'expert'), may hold values from -0.125 to 0.125
- up_train: bfloat16 [16, 2048, 768], P(None, 'expert'), may hold values from -0.125 to 0.125
- down_train: bfloat16 [16, 768, 2048], P(None, 'expert'), may hold values from -0.21875 to 0.21875
Outputs:
- attended: bfloat16 [256, 4096], P(('groups', 'expert')), parts along dimension 0
- expert_mix: bfloat16 [2048, 2048], P(('groups', 'expert')), parts along dimension 0
There are 2 independent parts, one for each index of `groups`. A program takes and returns all parts, laid end to end along the dimension named above; an argument that names none is the same for every part. Nothing has to cross between parts.
Inputs may be any that keep to these rules, and one draw needn't show every extreme that they name: `expert_ids`: each row names 8 different experts; within the rows of one device no expert is named more than 64 times. `cache_lengths`: the first sequence of each device's 8 has all 64 positions filled.
All inputs are finite; a program needn't handle non-finite values.
Results may differ from a plain program's by a relative error of at most 0.0074.
Values may be sent and summed in bfloat16 or wider, within the bound.
A program may use at most 128 MiB of HBM per device.

v0:
```python
import math

import jax
import jax.numpy as jnp
from jax import lax
from jax.sharding import PartitionSpec as P

HEADS = 32
KV_HEADS = 4
HEAD_DIM = 128
CTX = 64


EPSILON = 1e-06


def rms_normed(hidden_in, norm_gain):
    values = hidden_in.astype(jnp.float32)
    mean_square = jnp.mean(values * values, axis=-1, keepdims=True)
    return (values * lax.rsqrt(mean_square + EPSILON) * norm_gain.astype(jnp.float32)).astype(
        jnp.bfloat16
    )


def attend(queries, key_cache, value_cache, new_key, new_value, cache_lengths):
    seq_count = queries.shape[0]
    group_size = HEADS // KV_HEADS
    query_blocks = queries.reshape(seq_count, KV_HEADS, group_size, HEAD_DIM)
    cached_keys = key_cache.reshape(seq_count, CTX, KV_HEADS, HEAD_DIM)
    cached_values = value_cache.reshape(seq_count, CTX, KV_HEADS, HEAD_DIM)
    fresh_keys = new_key.reshape(seq_count, KV_HEADS, HEAD_DIM)
    fresh_values = new_value.astype(jnp.float32).reshape(seq_count, KV_HEADS, HEAD_DIM)
    score_scale = 1.0 / math.sqrt(HEAD_DIM)
    scores = (
        jnp.einsum("sgrd,scgd->sgrc", query_blocks, cached_keys, preferred_element_type=jnp.float32)
        * score_scale
    )
    own_score = (
        jnp.einsum("sgrd,sgd->sgr", query_blocks, fresh_keys, preferred_element_type=jnp.float32)
        * score_scale
    )
    positions = jnp.arange(CTX, dtype=jnp.int32)
    visible = positions[None, :] < cache_lengths[:, None]
    scores = jnp.where(visible[:, None, None, :], scores, -1e30)
    largest = jnp.maximum(jnp.max(scores, axis=-1), own_score)
    cached_exp = jnp.exp(scores - largest[..., None])
    own_exp = jnp.exp(own_score - largest)
    prob_total = jnp.sum(cached_exp, axis=-1) + own_exp
    cached_prob = (cached_exp / prob_total[..., None]).astype(jnp.bfloat16)
    own_prob = (own_exp / prob_total).astype(jnp.bfloat16).astype(jnp.float32)
    context = jnp.einsum(
        "sgrc,scgd->sgrd", cached_prob, cached_values, preferred_element_type=jnp.float32
    )
    context = context + own_prob[..., None] * fresh_values[:, :, None, :]
    return context.reshape(seq_count, HEADS * HEAD_DIM).astype(jnp.bfloat16)


def expert_rows(received, gate_weight, up_weight, down_weight):
    token_rows = received.reshape(-1, received.shape[2])
    gate_proj = jnp.dot(token_rows, gate_weight, preferred_element_type=jnp.float32)
    up_proj = jnp.dot(token_rows, up_weight, preferred_element_type=jnp.float32)
    hidden_units = (jax.nn.silu(gate_proj) * up_proj).astype(jnp.bfloat16)
    expert_out = jnp.dot(hidden_units, down_weight, preferred_element_type=jnp.float32).astype(
        jnp.bfloat16
    )
    return lax.all_to_all(
        expert_out.reshape(received.shape), "expert", split_axis=0, concat_axis=0, tiled=True
    )


def local(
    queries,
    key_cache,
    value_cache,
    new_key,
    new_value,
    cache_lengths,
    hidden_in,
    norm_gain,
    router_weight,
    expert_ids,
    gate_train,
    up_train,
    down_train,
):
    gate_moved, up_moved, down_moved = (
        lax.all_to_all(gate_train, "expert", split_axis=0, concat_axis=1, tiled=True),
        lax.all_to_all(up_train, "expert", split_axis=0, concat_axis=1, tiled=True),
        lax.all_to_all(down_train, "expert", split_axis=0, concat_axis=1, tiled=True),
    )
    attended = attend(queries, key_cache, value_cache, new_key, new_value, cache_lengths)
    tok_count = hidden_in.shape[0]
    expert_count = router_weight.shape[1]
    top_count = expert_ids.shape[1]
    width = hidden_in.shape[1]
    slot_count = 2 * tok_count * top_count // expert_count
    normed = rms_normed(hidden_in, norm_gain)
    logits = jnp.dot(normed, router_weight, preferred_element_type=jnp.float32)
    expert_range = jnp.arange(expert_count, dtype=jnp.int32)
    picked = expert_ids[:, :, None] == expert_range[None, None, :]
    chosen = jnp.sum(jnp.where(picked, logits[:, None, :], 0.0), axis=-1)
    mixing = jax.nn.softmax(chosen, axis=-1)
    onehot_int = picked.astype(jnp.int32).reshape(-1, expert_count)
    rank_values = jnp.sum((jnp.cumsum(onehot_int, axis=0) - 1) * onehot_int, axis=-1)
    targets = expert_ids.reshape(-1) * slot_count + rank_values
    slot_range = jnp.arange(expert_count * slot_count, dtype=jnp.int32)
    placing = slot_range[:, None] == targets[None, :]
    all_rows, all_ids = (
        lax.all_gather(normed, "expert", axis=0, tiled=True),
        lax.all_gather(expert_ids, "expert", axis=0, tiled=True),
    )
    device_count = lax.axis_size("expert")
    own_index = lax.axis_index("expert")
    own_hits = (all_ids == own_index).astype(jnp.int32).reshape(device_count, tok_count * top_count)
    own_ranks = jnp.cumsum(own_hits, axis=1) - 1
    own_targets = jnp.where(own_hits > 0, own_ranks, -1)
    token_owner = jnp.arange(tok_count * top_count, dtype=jnp.int32) // top_count
    slot_steps = jnp.arange(slot_count, dtype=jnp.int32)
    matches = own_targets[:, None, :] == slot_steps[None, :, None]
    local_token = jnp.sum(jnp.where(matches, token_owner[None, None, :], 0), axis=-1)
    filled = jnp.any(matches, axis=-1)
    row_index = jnp.arange(device_count, dtype=jnp.int32)[:, None] * tok_count + local_token
    taken = jnp.take(all_rows, row_index.reshape(-1), axis=0).reshape(
        device_count, slot_count, width
    )
    received = jnp.where(filled[..., None], taken, jnp.zeros_like(taken))
    returned = expert_rows(received, gate_moved[0], up_moved[0], down_moved[0])
    flat_back = returned.reshape(expert_count * slot_count, width)
    per_assign = lax.dot_general(
        placing.astype(jnp.bfloat16),
        flat_back,
        (((0,), (0,)), ((), ())),
        preferred_element_type=jnp.float32,
    )
    mixed_out = jnp.sum(
        mixing[:, :, None] * per_assign.reshape(tok_count, top_count, width), axis=1
    ).astype(jnp.bfloat16)
    return (attended, mixed_out)


def solution(mesh):
    placed = (
        P(("groups", "expert"), None),
        P(("groups", "expert"), None, None),
        P(("groups", "expert"), None, None),
        P(("groups", "expert"), None),
        P(("groups", "expert"), None),
        P(("groups", "expert")),
        P(("groups", "expert"), None),
        P(),
        P(),
        P(("groups", "expert"), None),
        P(None, "expert", None),
        P(None, "expert", None),
        P(None, "expert", None),
    )
    return jax.shard_map(
        local,
        mesh=mesh,
        in_specs=placed,
        out_specs=(P(("groups", "expert"), None), P(("groups", "expert"), None)),
        check_vma=False,
    )
```

profile of v0, /device:TPU:13, one launch (start us, length us, event | category | flops | bytes accessed | tf_op | source)
XLA Modules:
  0.0 416.2 jit_solution(14784146556622299426)
XLA Ops:
  7.2 0.0 copy-start
  7.2 76.5 %all_to_all.32 = bf16[16,128,768]{2,1,0:T(8,128)(2,1)} all-to-all(bf16[16,128,768]{2,1,0:T(8,128)(2,1)} %param.23), channel_id=1, replica_groups=mesh['groups'=2,'expert'=16] {'expert'}, dimensions={0} | all-to-all | bytes 6291456 | tf_op jit(solution)/shard_map/all_to_all | solution.py:87
  83.7 0.0 copy-start.8
  83.7 0.0 copy-start.2
  83.7 5.2 %all-to-all-start.1 = ((bf16[16,128,768]{2,1,0:T(8,128)(2,1)}), bf16[16,128,768]{2,1,0:T(8,128)(2,1)}, u32[]{:S(2)}, u32[]{:S(2)}) async-start(bf16[16,128,768]{2,1,0:T(8,128)(2,1)} %param.24), calls=%async_computation.1 | async-start | bytes 6291456 | tf_op jit(solution)/shard_map/all_to_all | solution.py:88
  88.9 0.0 all-gather.3.cloned.1.call-start
  89.0 0.0 copy-done.8
  89.0 0.0 copy-done.2
  89.0 0.2 fusion.7
  89.2 0.8 fusion.9
  90.0 0.0 all-gather.3.cloned.1.call-update
  90.0 0.0 copy-start.6
  90.0 94.1 %all-to-all-done.1 = bf16[16,128,768]{2,1,0:T(8,128)(2,1)} async-done(((bf16[16,128,768]{2,1,0:T(8,128)(2,1)}), bf16[16,128,768]{2,1,0:T(8,128)(2,1)}, u32[]{:S(2)}, u32[]{:S(2)}) %all-to-all-start.1) | async-done | bytes 3145760 | tf_op jit(solution)/shard_map/all_to_all | solution.py:88
  184.2 4.8 %all-to-all-start.2 = ((bf16[16,48,2048]{2,1,0:T(8,128)(2,1)}), bf16[16,48,2048]{2,1,0:T(8,128)(2,1)}, u32[]{:S(2)}, u32[]{:S(2)}) async-start(bf16[16,48,2048]{2,1,0:T(8,128)(2,1)} %param.25), calls=%async_computation.2 | async-start | bytes 6291456 | tf_op jit(solution)/shard_map/all_to_all | solution.py:89
  189.0 0.0 copy-done.6
  189.0 79.5 %all-gather = s32[16,64,8]{1,2,0:T(8,128)S(1)} all-gather(s32[1,64,8]{1,2,0:T(8,128)S(1)} %bitcast.77), channel_id=1, replica_groups=mesh['groups'=2,'expert'=16] {'expert'}, dimensions={0}, use_global_device_ids=true | all-gather | bytes 34816 | tf_op jit(solution)/shard_map/all_gather | solution.py:110
  268.5 0.2 copy.59
  268.7 0.2 copy.60
  268.9 0.1 copy.61
  269.0 1.1 reduce-window.16
  270.1 0.2 slice_reduce_fusion
  270.4 0.1 add_add_fusion
  270.5 0.1 copy.67
  270.6 0.1 copy.64
  270.7 0.4 select_reduce_fusion
  271.1 0.1 broadcast_add_fusion
  271.2 0.1 add.101
  271.3 0.1 add.98
  271.3 0.4 fusion
  271.7 0.1 broadcast_in_dim.86
  271.8 0.0 all-gather.3.cloned.1.call-done
  271.9 11.6 %gather_fusion = bf16[1024,2048]{1,0:T(8,128)(2,1)} fusion(bf16[1024,2048]{1,0:T(8,128)(2,1)} %all-gather.3.cloned.1.call-done, s32[1024]{0:T(1024)S(1)} %broadcast_clamp_fusion), kind=kCustom, calls=%fused_computation | custom fusion | bytes 8392704 | tf_op jit(solution)/shard_map/jit(_take)/gather | solution.py:123
  283.4 8.3 %fusion.32 = f32[1024,768]{1,0:T(8,128)} fusion(bf16[2048,768]{1,0:T(8,128)(2,1)} %bitcast.70, bf16[1024,2048]{1,0:T(8,128)(2,1)} %gather_fusion, pred[1024]{0:T(1024)(128)(4,1)S(1)} %compare_and_fusion, pred[1024]{0:T(1024)(128)(4,1)S(1)} %broadcast_in_dim.86), kind=kOutput, calls=%fused_computation.76 | convolution fusion | flops 3225419776 | bytes 10487808 | tf_op jit(solution)/shard_map/dot_general | solution.py:60
  291.7 0.0 all-to-all-done.2
  291.7 13.6 %convolution_convert_fusion = bf16[1024,2048]{1,0:T(8,128)(2,1)} fusion(bf16[768,2048]{1,0:T(8,128)(2,1)} %bitcast.15, f32[1024,768]{1,0:T(8,128)} %fusion.32, bf16[2048,768]{1,0:T(8,128)(2,1)} %bitcast.14, bf16[1024,2048]{1,0:T(8,128)(2,1)} %gather_fusion, pred[1024]{0:T(1024)(128)(4,1)S(1)} %compare_and_fusion, pred[1024]{0:T(1024)(128)(4,1)S(1)} %broadcast_in_dim.86), kind=kOutput, calls=%fused_computation.3 | convolution fusion | flops 6453460992 | bytes 17827840 | tf_op jit(solution)/shard_map/dot_general | solution.py:63
  305.3 0.0 copy-start.7
  305.3 0.0 copy-start.9
  305.3 0.0 copy-start.3
  305.3 5.1 %all-to-all-start.3 = ((bf16[16,64,2048]{2,1,0:T(8,128)(2,1)}), bf16[16,64,2048]{2,1,0:T(8,128)(2,1)}, u32[]{:S(2)}, u32[]{:S(2)}) async-start(bf16[16,64,2048]{2,1,0:T(8,128)(2,1)} %bitcast.69), calls=%async_computation.3 | async-start | bytes 8388608 | tf_op jit(solution)/shard_map/all_to_all | solution.py:66
  310.4 0.0 copy-start.5
  310.4 0.1 copy.56
  310.5 0.1 reshape.285
  310.6 0.1 eq.78
  310.7 0.0 copy-done.7
  310.8 1.2 reduce-window.14
  311.9 0.2 slice_reduce_fusion.1
  312.2 0.0 copy-done.10
  312.2 0.1 iota_compare_fusion.5
  312.2 0.0 copy-done.4
  312.3 0.0 copy-done.9
  312.3 0.2 fusion.17
  312.4 0.0 copy-done.3
  312.4 0.5 fusion.33
  312.9 0.2 fusion.14
  313.2 0.0 copy-done
  313.2 0.3 fusion.5
  313.5 0.7 copy.93
  314.2 0.0 copy-done.1
  314.2 0.0 copy-done.5
  314.2 0.2 fusion.34
  314.4 0.1 copy.55
  314.5 0.1 fusion.21
  314.6 88.7 %all-to-all-done.3 = bf16[16,64,2048]{2,1,0:T(8,128)(2,1)} async-done(((bf16[16,64,2048]{2,1,0:T(8,128)(2,1)}), bf16[16,64,2048]{2,1,0:T(8,128)(2,1)}, u32[]{:S(2)}, u32[]{:S(2)}) %all-to-all-start.3) | async-done | bytes 4194336 | tf_op jit(solution)/shard_map/all_to_all | solution.py:66
  403.4 6.0 %multiply_reduce_fusion = bf16[64,2048]{1,0:T(8,128)(2,1)} fusion(bf16[1024,2048,1]{1,0,2:T(8,128)(2,1)} %bitcast.18, f32[64,8]{1,0:T(8,128)S(1)} %copy.55, s32[512]{0:T(512)S(1)} %multiply_add_fusion), kind=kOutput, calls=%fused_computation.1 | convolution fusion | flops 2149974016 | bytes 4460544 | tf_op jit(solution)/shard_map/dot_general | solution.py:129
  (26 shorter events, 0.3 us)
Async XLA Ops:
  7.2 306.0 %copy-start = (bf16[8,64,512]{2,1,0:T(8,128)(2,1)S(1)}, bf16[8,64,512]{2,1,0:T(8,128)(2,1)}, u32[]{:S(2)}) copy-start(bf16[8,64,512]{2,1,0:T(8,128)(2,1)} %param.15) | copy-start | bytes 1572868
  83.7 5.3 %copy-start.8 = (bf16[2048]{0:T(1024)(128)(2,1)S(1)}, bf16[2048]{0:T(1024)(128)(2,1)}, u32[]{:S(2)}) copy-start(bf16[2048]{0:T(1024)(128)(2,1)} %param.20) | copy-start | bytes 12292
  83.7 5.3 %copy-start.2 = (bf16[64,2048]{1,0:T(8,128)(2,1)S(1)}, bf16[64,2048]{1,0:T(8,128)(2,1)}, u32[]{:S(2)}) copy-start(bf16[64,2048]{1,0:T(8,128)(2,1)} %param.19) | copy-start | bytes 786436
  83.7 100.5 %all-to-all-start.1 = ((bf16[16,128,768]{2,1,0:T(8,128)(2,1)}), bf16[16,128,768]{2,1,0:T(8,128)(2,1)}, u32[]{:S(2)}, u32[]{:S(2)}) async-start(bf16[16,128,768]{2,1,0:T(8,128)(2,1)} %param.24), calls=%async_computation.1 | async-start | bytes 6291456 | tf_op jit(solution)/shard_map/all_to_all | solution.py:88
  88.9 182.9 %all-gather.3.cloned.1.call-start = ((), (), s32[]{:S(2)}) async-start(), calls=%async_computation.4 | async-start | bytes 4456448 | tf_op jit(solution)/shard_map/all_gather | solution.py:109
  90.0 99.0 %copy-start.6 = (s32[64,8]{0,1:T(8,128)S(1)}, s32[64,8]{0,1:T(8,128)}, u32[]{:S(2)}) copy-start(s32[64,8]{0,1:T(8,128)} %param.22) | copy-start | bytes 6148
  184.2 107.5 %all-to-all-start.2 = ((bf16[16,48,2048]{2,1,0:T(8,128)(2,1)}), bf16[16,48,2048]{2,1,0:T(8,128)(2,1)}, u32[]{:S(2)}, u32[]{:S(2)}) async-start(bf16[16,48,2048]{2,1,0:T(8,128)(2,1)} %param.25), calls=%async_computation.2 | async-start | bytes 6291456 | tf_op jit(solution)/shard_map/all_to_all | solution.py:89
  305.3 5.4 %copy-start.7 = (bf16[8,512]{1,0:T(8,128)(2,1)S(1)}, bf16[8,512]{1,0:T(8,128)(2,1)}, u32[]{:S(2)}) copy-start(bf16[8,512]{1,0:T(8,128)(2,1)} %param.17) | copy-start | bytes 24580
  305.3 6.9 %copy-start.10 = (s32[8]{0:T(128)S(1)}, s32[8]{0:T(128)}, u32[]{:S(2)}) copy-start(s32[8]{0:T(128)} %param.18) | copy-start | bytes 100
  305.3 7.0 %copy-start.4 = (bf16[8,4096]{1,0:T(8,128)(2,1)S(1)}, bf16[8,4096]{1,0:T(8,128)(2,1)}, u32[]{:S(2)}) copy-start(bf16[8,4096]{1,0:T(8,128)(2,1)} %param.13) | copy-start | bytes 196612
  305.3 7.0 %copy-start.9 = (bf16[8,512]{1,0:T(8,128)(2,1)S(1)}, bf16[8,512]{1,0:T(8,128)(2,1)}, u32[]{:S(2)}) copy-start(bf16[8,512]{1,0:T(8,128)(2,1)} %param.16) | copy-start | bytes 24580
  305.3 7.1 %copy-start.3 = (bf16[8,64,512]{2,1,0:T(8,128)(2,1)S(1)}, bf16[8,64,512]{2,1,0:T(8,128)(2,1)}, u32[]{:S(2)}) copy-start(bf16[8,64,512]{2,1,0:T(8,128)(2,1)} %param.14) | copy-start | bytes 1572868
  305.3 98.1 %all-to-all-start.3 = ((bf16[16,64,2048]{2,1,0:T(8,128)(2,1)}), bf16[16,64,2048]{2,1,0:T(8,128)(2,1)}, u32[]{:S(2)}, u32[]{:S(2)}) async-start(bf16[16,64,2048]{2,1,0:T(8,128)(2,1)} %bitcast.69), calls=%async_computation.3 | async-start | bytes 8388608 | tf_op jit(solution)/shard_map/all_to_all | solution.py:66
  310.4 3.7 copy-start.1
  310.4 3.7 copy-start.5
Sparse Core Ops, SparseCore 0:
  92.5 77.4 all-gather.2
where the time goes:
time: 417 us; the launch traced here: 416 us
  waiting for transfers between devices  183 us (44%)
  blocking collectives  156 us (37%)
  matrix products  28.9 us (7%)
  starting transfers between devices  15.2 us (4%)
  between operations  14.3 us (3%)
  local copies, waits for them, and re-layouts  14 us (3%)
  other arithmetic  4.86 us (1%)
    all_to_all x1, waiting for transfers between devices, local(): lax.all_to_all(up_train, 'expert', split_axis=0, concat_axis=1, tiled=True)  94.1 us
    all_to_all x1, waiting for transfers between devices, expert_rows(): lax.all_to_all(expert_out.reshape(received.shape), 'expert', split_axis=0...  88.7 us
    all_gather x1, blocking collectives, local(): lax.all_gather(expert_ids, 'expert', axis=0, tiled=True)  79.5 us
    all_to_all x1, blocking collectives, local(): lax.all_to_all(gate_train, 'expert', split_axis=0, concat_axis=1, tiled=T...  76.5 us
    dot_general x1, matrix products, expert_rows(): jnp.dot(hidden_units, down_weight, preferred_element_type=jnp.float32)  13.6 us
    gather x1, local copies, waits for them, and re-layouts, local(): jnp.take(all_rows, row_index.reshape(-1), axis=0)  11.6 us
  transfers between devices with their start and end apart: 4, of which 2 were waited for; matrix products, arithmetic and copies ran while one was open for 7% of the time, Pallas kernels for 0%

commit v1 on v0

v1 whole, which is shorter than its diff:
```python
import math

import jax
import jax.numpy as jnp
from jax import lax
from jax.sharding import PartitionSpec as P

HEADS = 32
KV_HEADS = 4
HEAD_DIM = 128
CTX = 64


EPSILON = 1e-06


def rms_normed(hidden_in, norm_gain):
    values = hidden_in.astype(jnp.float32)
    mean_square = jnp.mean(values * values, axis=-1, keepdims=True)
    return (values * lax.rsqrt(mean_square + EPSILON) * norm_gain.astype(jnp.float32)).astype(
        jnp.bfloat16
    )


def attend(queries, key_cache, value_cache, new_key, new_value, cache_lengths):
    seq_count = queries.shape[0]
    group_size = HEADS // KV_HEADS
    query_blocks = queries.reshape(seq_count, KV_HEADS, group_size, HEAD_DIM)
    cached_keys = key_cache.reshape(seq_count, CTX, KV_HEADS, HEAD_DIM)
    cached_values = value_cache.reshape(seq_count, CTX, KV_HEADS, HEAD_DIM)
    fresh_keys = new_key.reshape(seq_count, KV_HEADS, HEAD_DIM)
    fresh_values = new_value.astype(jnp.float32).reshape(seq_count, KV_HEADS, HEAD_DIM)
    score_scale = 1.0 / math.sqrt(HEAD_DIM)
    scores = (
        jnp.einsum("sgrd,scgd->sgrc", query_blocks, cached_keys, preferred_element_type=jnp.float32)
        * score_scale
    )
    own_score = (
        jnp.einsum("sgrd,sgd->sgr", query_blocks, fresh_keys, preferred_element_type=jnp.float32)
        * score_scale
    )
    positions = jnp.arange(CTX, dtype=jnp.int32)
    visible = positions[None, :] < cache_lengths[:, None]
    scores = jnp.where(visible[:, None, None, :], scores, -1e30)
    largest = jnp.maximum(jnp.max(scores, axis=-1), own_score)
    cached_exp = jnp.exp(scores - largest[..., None])
    own_exp = jnp.exp(own_score - largest)
    prob_total = jnp.sum(cached_exp, axis=-1) + own_exp
    cached_prob = (cached_exp / prob_total[..., None]).astype(jnp.bfloat16)
    own_prob = (own_exp / prob_total).astype(jnp.bfloat16).astype(jnp.float32)
    context = jnp.einsum(
        "sgrc,scgd->sgrd", cached_prob, cached_values, preferred_element_type=jnp.float32
    )
    context = context + own_prob[..., None] * fresh_values[:, :, None, :]
    return context.reshape(seq_count, HEADS * HEAD_DIM).astype(jnp.bfloat16)


def dense_mixing(normed, router_weight, expert_ids):
    logits = jnp.dot(normed, router_weight, preferred_element_type=jnp.float32)
    expert_range = jnp.arange(router_weight.shape[1], dtype=jnp.int32)
    picked = jnp.any(expert_ids[:, :, None] == expert_range[None, None, :], axis=1)
    masked = jnp.where(picked, logits, -jnp.inf)
    raised = jnp.exp(masked - jnp.max(masked, axis=-1, keepdims=True))
    return raised / jnp.sum(raised, axis=-1, keepdims=True)


def local(
    queries,
    key_cache,
    value_cache,
    new_key,
    new_value,
    cache_lengths,
    hidden_in,
    norm_gain,
    router_weight,
    expert_ids,
    gate_train,
    up_train,
    down_train,
):
    width = hidden_in.shape[1]
    expert_count = router_weight.shape[1]
    normed = rms_normed(hidden_in, norm_gain)
    mixing = dense_mixing(normed, router_weight, expert_ids)
    mixing_high = mixing.astype(jnp.bfloat16)
    mixing_low = (mixing - mixing_high.astype(jnp.float32)).astype(jnp.bfloat16)
    spare = -2 * expert_count % 128
    row_block = jnp.concatenate(
        [normed, mixing_high, mixing_low, jnp.zeros((normed.shape[0], spare), jnp.bfloat16)], axis=1
    )
    all_rows = lax.all_gather(row_block, "expert", axis=0, tiled=True)
    gate_moved = lax.all_to_all(gate_train, "expert", split_axis=0, concat_axis=1, tiled=True)[0]
    up_moved = lax.all_to_all(up_train, "expert", split_axis=0, concat_axis=1, tiled=True)[0]
    attended = attend(queries, key_cache, value_cache, new_key, new_value, cache_lengths)
    own_index = lax.axis_index("expert")
    tokens = all_rows[:, :width]
    mix_parts = all_rows[:, width : width + 2 * expert_count].astype(jnp.float32)
    own_column = jnp.arange(2 * expert_count) % expert_count == own_index
    own_mix = jnp.sum(jnp.where(own_column[None, :], mix_parts, 0.0), axis=1)
    contract = (((0,), (1,)), ((), ()))
    gate_proj = lax.dot_general(gate_moved, tokens, contract, preferred_element_type=jnp.float32)
    up_proj = lax.dot_general(up_moved, tokens, contract, preferred_element_type=jnp.float32)
    hidden_units = (jax.nn.silu(gate_proj) * up_proj * own_mix[None, :]).astype(jnp.bfloat16)
    hidden_all = lax.all_to_all(hidden_units, "expert", split_axis=0, concat_axis=0, tiled=True)
    partial_out = lax.dot_general(
        hidden_all,
        down_train.reshape(-1, width),
        (((0,), (0,)), ((), ())),
        preferred_element_type=jnp.float32,
    ).astype(jnp.bfloat16)
    mixed_out = lax.psum_scatter(partial_out, "expert", scatter_dimension=0, tiled=True)
    return (attended, mixed_out)


def solution(mesh):
    placed = (
        P(("groups", "expert"), None),
        P(("groups", "expert"), None, None),
        P(("groups", "expert"), None, None),
        P(("groups", "expert"), None),
        P(("groups", "expert"), None),
        P(("groups", "expert")),
        P(("groups", "expert"), None),
        P(),
        P(),
        P(("groups", "expert"), None),
        P(None, "expert", None),
        P(None, "expert", None),
        P(None, "expert", None),
    )
    return jax.shard_map(
        local,
        mesh=mesh,
        in_specs=placed,
        out_specs=(P(("groups", "expert"), None), P(("groups", "expert"), None)),
        check_vma=False,
    )
```

time: 417 us -> 321 us (0.77)
  the two profiles are of different devices: /device:TPU:13 before, /device:TPU:0 now
where the time goes in v1:
time: 321 us; the launch traced here: 320 us
  waiting for transfers between devices  202 us (63%)
  blocking collectives  51.1 us (16%)
  matrix products  24.7 us (8%)
  starting transfers between devices  23.4 us (7%)
  between operations  14.2 us (4%)
    all_to_all x1, waiting for transfers between devices, local(): lax.all_to_all(gate_train, 'expert', split_axis=0, concat_axis=1, tiled=T...  83.3 us
    reduce_scatter x1, waiting for transfers between devices, local(): lax.psum_scatter(partial_out, 'expert', scatter_dimension=0, tiled=True)  68.5 us
    all_to_all x1, blocking collectives, local(): lax.all_to_all(hidden_units, 'expert', split_axis=0, concat_axis=0, tiled...  51.1 us
    all_to_all x1, waiting for transfers between devices, local(): lax.all_to_all(up_train, 'expert', split_axis=0, concat_axis=1, tiled=True)  49.7 us
    all_to_all x1, starting transfers between devices, local(): lax.all_to_all(up_train, 'expert', split_axis=0, concat_axis=1, tiled=True)  15.6 us
    dot_general x1, matrix products, local(): lax.dot_general(gate_moved, tokens, contract, preferred_element_type=jnp....  8.42 us
    dot_general x1, matrix products, local(): lax.dot_general(up_moved, tokens, contract, preferred_element_type=jnp.fl...  8.02 us
    all_to_all x1, starting transfers between devices, local(): lax.all_to_all(gate_train, 'expert', split_axis=0, concat_axis=1, tiled=T...  7.73 us
  transfers between devices with their start and end apart: 4, of which 3 were waited for; matrix products, arithmetic and copies ran while one was open for 5% of the time, Pallas kernels for 0%

profile of v1, /device:TPU:0, one launch (start us, length us, event | category | flops | bytes accessed | tf_op | source)
XLA Modules:
  0.0 320.3 jit_solution(8973925862852582639)
XLA Ops:
  7.2 0.0 copy-start
  7.2 0.0 copy-start.5
  7.2 0.0 copy-start.6
  7.2 0.0 copy-start.1
  7.2 0.0 copy-start.3
  7.2 7.7 %all-to-all-start = ((bf16[16,128,768]{2,1,0:T(8,128)(2,1)}), bf16[16,128,768]{2,1,0:T(8,128)(2,1)}, u32[]{:S(2)}, u32[]{:S(2)}) async-start(bf16[16,128,768]{2,1,0:T(8,128)(2,1)} %param.23), calls=%async_computation | async-start | bytes 6291456 | tf_op jit(solution)/shard_map/all_to_all | solution.py:93
  15.0 0.0 all-gather.2.cloned.1.call-start
  15.0 0.0 copy-done.5
  15.0 0.0 copy-done.6
  15.1 0.0 copy-done.1
  15.1 0.2 fusion.14
  15.2 1.1 fusion.16
  16.3 0.0 copy-done.3
  16.3 0.2 fusion.36
  16.6 0.1 copy.26
  16.7 0.1 copy.27
  16.8 0.8 concatenate.3
  17.6 0.0 all-gather.2.cloned.1.call-update
  17.7 83.3 %all-to-all-done = bf16[16,128,768]{2,1,0:T(8,128)(2,1)} async-done(((bf16[16,128,768]{2,1,0:T(8,128)(2,1)}), bf16[16,128,768]{2,1,0:T(8,128)(2,1)}, u32[]{:S(2)}, u32[]{:S(2)}) %all-to-all-start) | async-done | bytes 3145760 | tf_op jit(solution)/shard_map/all_to_all | solution.py:93
  101.0 15.6 %all-to-all-start.1 = ((bf16[16,128,768]{2,1,0:T(8,128)(2,1)}), bf16[16,128,768]{2,1,0:T(8,128)(2,1)}, u32[]{:S(2)}, u32[]{:S(2)}) async-start(bf16[16,128,768]{2,1,0:T(8,128)(2,1)} %param.24), calls=%async_computation.1 | async-start | bytes 6291456 | tf_op jit(solution)/shard_map/all_to_all | solution.py:94
  116.6 0.0 reduce-scatter.2.cloned.1.call-start
  116.6 0.0 all-gather.2.cloned.1.call-done
  116.7 1.1 select_reduce_fusion
  117.8 8.4 %fusion.2 = f32[1024,768]{0,1:T(8,128)} fusion(bf16[2048,768]{1,0:T(8,128)(2,1)} %bitcast.6, bf16[1024,2176]{1,0:T(8,128)(2,1)} %all-gather.2.cloned.1.call-done), kind=kOutput, calls=%fused_computation.3 | convolution fusion | flops 3221225472 | bytes 10485760 | tf_op jit(solution)/shard_map/dot_general | solution.py:102
  126.2 49.7 %all-to-all-done.1 = bf16[16,128,768]{2,1,0:T(8,128)(2,1)} async-done(((bf16[16,128,768]{2,1,0:T(8,128)(2,1)}), bf16[16,128,768]{2,1,0:T(8,128)(2,1)}, u32[]{:S(2)}, u32[]{:S(2)}) %all-to-all-start.1) | async-done | bytes 3145760 | tf_op jit(solution)/shard_map/all_to_all | solution.py:94
  175.9 8.0 %fusion.5 = bf16[768,1024]{1,0:T(8,128)(2,1)S(1)} fusion(f32[1024,768]{0,1:T(8,128)} %fusion.2, bf16[2048,768]{1,0:T(8,128)(2,1)} %bitcast.8, bf16[1024,2176]{1,0:T(8,128)(2,1)} %all-gather.2.cloned.1.call-done, f32[1024]{0:T(1024)S(1)} %select_reduce_fusion), kind=kOutput, calls=%fused_computation.7 | convolution fusion | flops 3226730496 | bytes 12062720 | tf_op jit(solution)/shard_map/dot_general | solution.py:103
  183.9 51.1 %all_to_all.27 = bf16[16,48,1024]{2,1,0:T(8,128)(2,1)S(1)} all-to-all(bf16[16,48,1024]{2,1,0:T(8,128)(2,1)S(1)} %bitcast.61), channel_id=1, replica_groups=mesh['groups'=2,'expert'=16] {'expert'}, dimensions={0} | all-to-all | bytes 3145728 | tf_op jit(solution)/shard_map/all_to_all | solution.py:105
  235.0 0.0 copy-done
  235.0 5.0 %bitcast_convert_fusion = bf16[1024,2048]{1,0:T(8,128)(2,1)} fusion(bf16[16,48,1024]{2,1,0:T(8,128)(2,1)S(1)} %all_to_all.27, bf16[16,48,2048]{2,1,0:T(8,128)(2,1)S(1)} %copy-done), kind=kOutput, calls=%fused_computation | convolution fusion | flops 3223322624 | bytes 8912896 | tf_op jit(solution)/shard_map/dot_general | solution.py:106
  240.1 0.0 copy-start.4
  240.1 0.0 copy-start.8
  240.1 0.0 copy-start.2
  240.1 0.0 copy-start.7
  240.1 0.0 reduce-scatter.2.cloned.1.call-update
  240.1 0.7 copy-done.4
  240.8 0.0 copy-done.8
  240.8 0.1 iota_compare_fusion.1
  240.9 0.1 copy-done.2
  240.9 0.0 copy-done.7
  241.0 0.2 fusion.25
  241.1 1.5 fusion.35
  242.6 0.2 fusion.21
  242.9 1.4 fusion.13
  244.3 0.7 copy.52
  244.9 68.5 %reduce-scatter.2.cloned.1.call-done = bf16[64,2048]{1,0:T(8,128)(2,1)} async-done(((bf16[1024,2048]{1,0:T(8,128)(2,1)}), bf16[64,2048]{1,0:T(8,128)(2,1)}) %reduce-scatter.2.cloned.1.call-update) | async-done | bytes 262160 | tf_op jit(solution)/shard_map/reduce_scatter | solution.py:112
  (11 shorter events, 0.1 us)
Async XLA Ops:
  7.2 227.9 %copy-start = (bf16[16,48,2048]{2,1,0:T(8,128)(2,1)S(1)}, bf16[16,48,2048]{2,1,0:T(8,128)(2,1)}, u32[]{:S(2)}) copy-start(bf16[16,48,2048]{2,1,0:T(8,128)(2,1)} %param.25) | copy-start | bytes 9437188
  7.2 7.8 %copy-start.5 = (bf16[2048]{0:T(1024)(128)(2,1)S(1)}, bf16[2048]{0:T(1024)(128)(2,1)}, u32[]{:S(2)}) copy-start(bf16[2048]{0:T(1024)(128)(2,1)} %param.20) | copy-start | bytes 12292
  7.2 7.8 %copy-start.6 = (s32[64,8]{0,1:T(8,128)S(1)}, s32[64,8]{0,1:T(8,128)}, u32[]{:S(2)}) copy-start(s32[64,8]{0,1:T(8,128)} %param.22) | copy-start | bytes 6148
  7.2 7.9 %copy-start.1 = (bf16[64,2048]{1,0:T(8,128)(2,1)S(1)}, bf16[64,2048]{1,0:T(8,128)(2,1)}, u32[]{:S(2)}) copy-start(bf16[64,2048]{1,0:T(8,128)(2,1)} %param.19) | copy-start | bytes 786436
  7.2 9.1 %copy-start.3 = (bf16[2048,16]{0,1:T(8,128)(2,1)S(1)}, bf16[2048,16]{0,1:T(8,128)(2,1)}, u32[]{:S(2)}) copy-start(bf16[2048,16]{0,1:T(8,128)(2,1)} %param.21) | copy-start | bytes 196612
  7.2 93.8 %all-to-all-start = ((bf16[16,128,768]{2,1,0:T(8,128)(2,1)}), bf16[16,128,768]{2,1,0:T(8,128)(2,1)}, u32[]{:S(2)}, u32[]{:S(2)}) async-start(bf16[16,128,768]{2,1,0:T(8,128)(2,1)} %param.23), calls=%async_computation | async-start | bytes 6291456 | tf_op jit(solution)/shard_map/all_to_all | solution.py:93
  15.0 101.7 %all-gather.2.cloned.1.call-start = ((), (), s32[]{:S(2)}) async-start(), calls=%async_computation.4 | async-start | bytes 4734976 | tf_op jit(solution)/shard_map/all_gather | solution.py:92
  101.0 74.9 %all-to-all-start.1 = ((bf16[16,128,768]{2,1,0:T(8,128)(2,1)}), bf16[16,128,768]{2,1,0:T(8,128)(2,1)}, u32[]{:S(2)}, u32[]{:S(2)}) async-start(bf16[16,128,768]{2,1,0:T(8,128)(2,1)} %param.24), calls=%async_computation.1 | async-start | bytes 6291456 | tf_op jit(solution)/shard_map/all_to_all | solution.py:94
  116.6 196.9 %reduce-scatter.2.cloned.1.call-start = ((), (), s32[]{:S(2)}) async-start(), calls=%async_computation.5 | async-start | bytes 4456448 | tf_op jit(solution)/shard_map/reduce_scatter | solution.py:112
  240.1 0.7 copy-start.4
  240.1 0.7 copy-start.8
  240.1 0.9 copy-start.2
  240.1 0.9 copy-start.7
Sparse Core Ops, SparseCore 0:
  18.1 82.0 all-gather.1
  240.2 73.1 reduce-scatter.1

commit v2 on v1

--- a/solution.py
+++ b/solution.py
@@ -1,8 +1,11 @@
+import functools
 import math
 
 import jax
 import jax.numpy as jnp
 from jax import lax
+from jax.experimental import pallas as pl
+from jax.experimental.pallas import tpu as pltpu
 from jax.sharding import PartitionSpec as P
 
 HEADS = 32
@@ -62,6 +65,368 @@
     masked = jnp.where(picked, logits, -jnp.inf)
     raised = jnp.exp(masked - jnp.max(masked, axis=-1, keepdims=True))
     return raised / jnp.sum(raised, axis=-1, keepdims=True)
+
+
+MESH = pl.DeviceIdType.MESH
+AHEAD = 8
+
+
+def greet(targets):
+    barrier = pltpu.get_barrier_semaphore()
+
+    expected = 0
+    for condition, target in targets:
+        signal = functools.partial(
+            pl.semaphore_signal, barrier, inc=1, device_id=target, device_id_type=MESH
+        )
+        if condition is None:
+            signal()
+            expected = expected + 1
+        else:
+            pl.when(condition)(signal)
+            expected = expected + condition.astype(jnp.int32)
+    pl.semaphore_wait(barrier, expected)
+
+
+def move_kernel(
+    groups, count,
+    gate_ref, up_ref, down_ref, rows_ref,
+    gate_out, up_out, down_out, rows_out,
+    send_w, recv_w, send_x, recv_x, local_sem, send_rows, recv_rows,
+):
+    me = lax.axis_index("expert")
+    group = lax.axis_index("groups")
+    parts = max(1, groups // 2)
+    part_rows = gate_ref.shape[1] // parts
+    part_columns = down_ref.shape[2] // groups
+    line = count // 4
+    layer = me // 4
+
+    others = [(None, (group, me ^ r)) for r in range(1, count)]
+    others += [(None, (lax.rem(group + h, groups), me)) for h in range(1, groups)]
+    greet(others)
+
+    def remote(src, dst, send, recv, target):
+        return pltpu.make_async_remote_copy(
+            src_ref=src, dst_ref=dst, send_sem=send, recv_sem=recv, device_id=target, device_id_type=MESH
+        )
+
+    def rows_of(owner):
+        return pl.ds(pl.multiple_of((owner // 2) * part_rows, part_rows), part_rows)
+
+    def columns_of(owner):
+        return pl.ds(pl.multiple_of(owner * part_columns, part_columns), part_columns)
+
+    def row_copy(kind, block, target, own=False):
+        source = rows_ref if own else rows_out.at[block]
+        return remote(
+            source, rows_out.at[block], send_rows.at[kind, block], recv_rows.at[block], (group, target)
+        )
+
+    def row_wait(block):
+        row_copy(0, block, me ^ 1).wait_recv()
+
+    own_rows = pltpu.make_async_copy(rows_ref, rows_out.at[me], local_sem.at[3])
+    own_rows.start()
+    has_up, has_down = me + 4 < count, me >= 4
+
+    @pl.when(has_up)
+    def _():
+        row_copy(0, me, me + 4, True).start()
+
+    @pl.when(has_down)
+    def _():
+        row_copy(1, me, me - 4, True).start()
+
+    row_copy(2, me, me ^ 2, True).start()
+    row_copy(3, me, me ^ 1, True).start()
+
+    def line_step(step):
+        below, above = me - 4 * (step + 1), me + 4 * (step + 1)
+
+        @pl.when(below >= 0)
+        def _():
+            row_wait(below)
+
+            @pl.when(has_up)
+            def _():
+                row_copy(0, below, me + 4).start()
+
+            row_copy(2, below, me ^ 2).start()
+            row_copy(3, below, me ^ 1).start()
+
+        @pl.when(above < count)
+        def _():
+            row_wait(above)
+
+            @pl.when(has_down)
+            def _():
+                row_copy(1, above, me - 4).start()
+
+            row_copy(2, above, me ^ 2).start()
+            row_copy(3, above, me ^ 1).start()
+
+    def side_step(index):
+        block = lax.rem(me, 4) ^ 2
+        block = block + 4 * index
+        row_wait(block)
+        row_copy(3, block, me ^ 1).start()
+
+    def across(kind, r, refs_in, refs_out, which):
+        target = me ^ r
+        if kind == 0:
+            return remote(
+                refs_in[which].at[target, rows_of(group)], refs_out[which].at[me, rows_of(group)],
+                send_w.at[0, r], recv_w.at[0, r], (group, target),
+            )
+        return remote(
+            down_ref.at[target, :, columns_of(group)], down_out.at[me, :, columns_of(group)],
+            send_w.at[1, r], recv_w.at[1, r], (group, target),
+        )
+
+    ins, outs = (gate_ref, up_ref), (gate_out, up_out)
+
+    def by_matrix(act):
+        pl.when(lax.rem(group, 2) == 0)(functools.partial(act, 0))
+        pl.when(lax.rem(group, 2) == 1)(functools.partial(act, 1))
+
+    def start_weight(kind, r):
+        if kind == 0:
+            by_matrix(lambda which: across(0, r, ins, outs, which).start())
+        else:
+            across(1, r, ins, outs, 0).start()
+
+    def onward(kind, r, h, which):
+        held = me ^ r
+        place = outs[which].at[held, rows_of(group)] if kind == 0 else down_out.at[held, :, columns_of(group)]
+        return remote(
+            place, place, send_x.at[kind, r, h - 1], recv_x.at[kind, r, h - 1],
+            (lax.rem(group + h, groups), me),
+        )
+
+    def pass_on(kind, r):
+        across(kind, r, ins, outs, 0).wait_recv()
+        for h in range(1, groups):
+            if kind == 0:
+                by_matrix(lambda which: onward(0, r, h, which).start())
+            else:
+                onward(1, r, h, 0).start()
+
+    own_copies = [
+        pltpu.make_async_copy(a.at[me], b.at[me], local_sem.at[i])
+        for i, (a, b) in enumerate(((gate_ref, gate_out), (up_ref, up_out), (down_ref, down_out)))
+    ]
+    half = count // 2
+    order = [r for i in range(half) for r in ((half + i, i) if i else (half,))]
+    items = [(kind, r) for kind in range(2) for r in order]
+    side_at = 3 + 2 * (line - 1) + 2
+    for i, item in enumerate(items):
+        start_weight(*item)
+        if i >= 3 and (i - 3) % 2 == 0 and (i - 3) // 2 < line - 1:
+            line_step((i - 3) // 2)
+        if i == side_at:
+            for index in range(line):
+                side_step(index)
+        if i == AHEAD:
+            for copy in own_copies:
+                copy.start()
+        if i >= AHEAD:
+            pass_on(*items[i - AHEAD])
+    for item in items[len(items) - AHEAD :]:
+        pass_on(*item)
+
+    for index in range(line):
+        for y in range(2):
+            row_wait(4 * index + 2 * y + (lax.rem(me, 2) ^ 1))
+    own_rows.wait()
+    for copy in own_copies:
+        copy.wait()
+    for kind, r in items:
+        across(kind, r, ins, outs, 0).wait_send()
+        for h in range(1, groups):
+            onward(kind, r, h, 0).wait()
+    for index in range(line):
+        block = lax.rem(me, 4) + 4 * index
+
+        @pl.when(jnp.logical_and(has_up, index <= layer))
+        def _():
+            row_copy(0, block, me ^ 1).wait_send()
+
+        @pl.when(jnp.logical_and(has_down, index >= layer))
+        def _():
+            row_copy(1, block, me ^ 1).wait_send()
+
+        row_copy(2, block, me ^ 1).wait_send()
+        row_copy(3, block, me ^ 1).wait_send()
+        row_copy(3, block ^ 2, me ^ 1).wait_send()
+
+
+def move(groups, gate_train, up_train, down_train, row_block):
+    count = gate_train.shape[0]
+    anywhere = pl.BlockSpec(memory_space=pl.ANY)
+    DMA = pltpu.SemaphoreType.DMA
+    return pl.pallas_call(
+        functools.partial(move_kernel, groups, count),
+        out_shape=[
+            jax.ShapeDtypeStruct(gate_train.shape, gate_train.dtype),
+            jax.ShapeDtypeStruct(up_train.shape, up_train.dtype),
+            jax.ShapeDtypeStruct(down_train.shape, down_train.dtype),
+            jax.ShapeDtypeStruct((count,) + row_block.shape, row_block.dtype),
+        ],
+        in_specs=[anywhere, anywhere, anywhere, pl.BlockSpec(memory_space=pltpu.VMEM)],
+        out_specs=[anywhere] * 4,
+        scratch_shapes=[
+            DMA((2, count)), DMA((2, count)),
+            DMA((2, count, max(1, groups - 1))), DMA((2, count, max(1, groups - 1))),
+            DMA((4,)), DMA((4, count)), DMA((count,)),
+        ],
+        compiler_params=pltpu.CompilerParams(collective_id=0, has_side_effects=True),
+    )(gate_train, up_train, down_train, row_block)
+
+
+def sum_kernel(
+    count, part_ref, out_ref, core_in, side_in, up_in, down_in, side_out, up_out, down_out,
+    core_send, core_recv, side_send, side_recv, up_send, up_recv, down_send, down_recv,
+):
+    me = lax.axis_index("expert")
+    group = lax.axis_index("groups")
+    line, layer = count // 4, me // 4
+    place = lax.rem(me, 4)
+    side, core = place // 2, lax.rem(place, 2)
+    has_up, has_down = me + 4 < count, me >= 4
+    greet([
+        (None, (group, me ^ 1)), (None, (group, me ^ 2)),
+        (has_up, (group, me + 4)), (has_down, (group, me - 4)),
+    ])
+    chunk = 16
+    row_count = part_ref.shape[1]
+
+    def remote(src, dst, send, recv, target):
+        return pltpu.make_async_remote_copy(
+            src_ref=src, dst_ref=dst, send_sem=send, recv_sem=recv, device_id=(group, target), device_id_type=MESH
+        )
+
+    def add(target, *sources):
+        @pl.loop(0, row_count // chunk)
+        def _(step):
+            rows = pl.ds(pl.multiple_of(step * chunk, chunk), chunk)
+            total = sources[0][rows, :].astype(jnp.float32)
+            for source in sources[1:]:
+                total = total + source[rows, :].astype(jnp.float32)
+            target[rows, :] = total.astype(target.dtype)
+
+    def core_copy(at, y):
+        slot = at * 2 + y
+        return remote(
+            part_ref.at[at * 4 + y * 2 + (core ^ 1)], core_in.at[slot], core_send.at[slot], core_recv.at[slot], me ^ 1
+        )
+
+    def side_copy(at):
+        return remote(side_out.at[at], side_in.at[at], side_send.at[at], side_recv.at[at], me ^ 2)
+
+    def up_copy(at):
+        return remote(up_out.at[at], up_in.at[at], up_send.at[at], up_recv.at[at], me + 4)
+
+    def down_copy(at):
+        return remote(down_out.at[at], down_in.at[at], down_send.at[at], down_recv.at[at], me - 4)
+
+    def in_order(act):
+        for d in range(line - 1, 0, -1):
+            pl.when(layer + d < line)(functools.partial(act, layer + d, 1))
+            pl.when(layer - d >= 0)(functools.partial(act, layer - d, -1))
+        act(layer, 0)
+
+    in_order(lambda at, way: core_copy(at, side ^ 1).start())
+    in_order(lambda at, way: core_copy(at, side).start())
+
+    def to_side(at, way):
+        core_copy(at, side ^ 1).wait_recv()
+        add(side_out.at[at], part_ref.at[at * 4 + (side ^ 1) * 2 + core], core_in.at[at * 2 + (side ^ 1)])
+        side_copy(at).start()
+
+    in_order(to_side)
+
+    def along(at, way):
+        core_copy(at, side).wait_recv()
+        side_copy(at).wait_recv()
+        mine = (part_ref.at[at * 4 + place], core_in.at[at * 2 + side], side_in.at[at])
+        if way == 1:
+            @pl.when(has_down)
+            def _():
+                up_copy(at).wait_recv()
+                add(up_out.at[at], *mine, up_in.at[at])
+
+            @pl.when(jnp.logical_not(has_down))
+            def _():
+                add(up_out.at[at], *mine)
+
+            up_copy(at).start()
+        elif way == -1:
+            @pl.when(has_up)
+            def _():
+                down_copy(at).wait_recv()
+                add(down_out.at[at], *mine, down_in.at[at])
+
+            @pl.when(jnp.logical_not(has_up))
+            def _():
+                add(down_out.at[at], *mine)
+
+            down_copy(at).start()
+        else:
+            @pl.when(has_down)
+            def _():
+                up_copy(at).wait_recv()
+
+            @pl.when(has_up)
+            def _():
+                down_copy(at).wait_recv()
+
+            both = jnp.logical_and(has_down, has_up)
+
+            @pl.when(both)
+            def _():
+                add(out_ref, *mine, up_in.at[at], down_in.at[at])
+
+            @pl.when(jnp.logical_and(has_down, jnp.logical_not(has_up)))
+            def _():
+                add(out_ref, *mine, up_in.at[at])
+
+            @pl.when(jnp.logical_and(has_up, jnp.logical_not(has_down)))
+            def _():
+                add(out_ref, *mine, down_in.at[at])
+
+            @pl.when(jnp.logical_not(jnp.logical_or(has_up, has_down)))
+            def _():
+                add(out_ref, *mine)
+
+    in_order(along)
+
+    def finish(at, way):
+        core_copy(at, side ^ 1).wait_send()
+        core_copy(at, side).wait_send()
+        side_copy(at).wait_send()
+        if way == 1:
+            up_copy(at).wait_send()
+        if way == -1:
+            down_copy(at).wait_send()
+
+    in_order(finish)
+
+
+def summed(partial_out, count):
+    rows, width = partial_out.shape[0] // count, partial_out.shape[1]
+    line = count // 4
+    DMA = pltpu.SemaphoreType.DMA
+    block = lambda amount: pltpu.VMEM((amount, rows, width), jnp.bfloat16)
+    return pl.pallas_call(
+        functools.partial(sum_kernel, count),
+        out_shape=jax.ShapeDtypeStruct((rows, width), jnp.bfloat16),
+        in_specs=[pl.BlockSpec(memory_space=pltpu.VMEM)],
+        out_specs=pl.BlockSpec(memory_space=pltpu.VMEM),
+        scratch_shapes=[block(count // 2)] + [block(line)] * 6
+        + [DMA((count // 2,)), DMA((count // 2,))] + [DMA((line,))] * 6,
+        compiler_params=pltpu.CompilerParams(collective_id=1, has_side_effects=True, vmem_limit_bytes=60 * 2**20),
+    )(partial_out.reshape(count, rows, width))
 
 
 def local(
@@ -89,27 +454,24 @@
     row_block = jnp.concatenate(
         [normed, mixing_high, mixing_low, jnp.zeros((normed.shape[0], spare), jnp.bfloat16)], axis=1
     )
-    all_rows = lax.all_gather(row_block, "expert", axis=0, tiled=True)
-    gate_moved = lax.all_to_all(gate_train, "expert", split_axis=0, concat_axis=1, tiled=True)[0]
-    up_moved = lax.all_to_all(up_train, "expert", split_axis=0, concat_axis=1, tiled=True)[0]
+    gate_moved, up_moved, down_moved, all_rows = move(
+        lax.axis_size("groups"), gate_train, up_train, down_train, row_block
+    )
+    all_rows = all_rows.reshape(-1, all_rows.shape[-1])
+    gate_moved = gate_moved.reshape(-1, gate_moved.shape[-1])
+    up_moved = up_moved.reshape(-1, up_moved.shape[-1])
+    down_moved = down_moved.reshape(-1, width)
     attended = attend(queries, key_cache, value_cache, new_key, new_value, cache_lengths)
     own_index = lax.axis_index("expert")
     tokens = all_rows[:, :width]
     mix_parts = all_rows[:, width : width + 2 * expert_count].astype(jnp.float32)
     own_column = jnp.arange(2 * expert_count) % expert_count == own_index
     own_mix = jnp.sum(jnp.where(own_column[None, :], mix_parts, 0.0), axis=1)
-    contract = (((0,), (1,)), ((), ()))
-    gate_proj = lax.dot_general(gate_moved, tokens, contract, preferred_element_type=jnp.float32)
-    up_proj = lax.dot_general(up_moved, tokens, contract, preferred_element_type=jnp.float32)
-    hidden_units = (jax.nn.silu(gate_proj) * up_proj * own_mix[None, :]).astype(jnp.bfloat16)
-    hidden_all = lax.all_to_all(hidden_units, "expert", split_axis=0, concat_axis=0, tiled=True)
-    partial_out = lax.dot_general(
-        hidden_all,
-        down_train.reshape(-1, width),
-        (((0,), (0,)), ((), ())),
-        preferred_element_type=jnp.float32,
-    ).astype(jnp.bfloat16)
-    mixed_out = lax.psum_scatter(partial_out, "expert", scatter_dimension=0, tiled=True)
+    gate_proj = jnp.dot(tokens, gate_moved, preferred_element_type=jnp.float32)
+    up_proj = jnp.dot(tokens, up_moved, preferred_element_type=jnp.float32)
+    hidden_units = (jax.nn.silu(gate_proj) * up_proj * own_mix[:, None]).astype(jnp.bfloat16)
+    partial_out = jnp.dot(hidden_units, down_moved, preferred_element_type=jnp.float32).astype(jnp.bfloat16)
+    mixed_out = summed(partial_out, expert_count)
     return (attended, mixed_out)
 
 

time: 321 us -> 233 us (0.73)
  waiting for transfers between devices: 202 us -> 0 us
  Pallas kernels: 0 us -> 200 us
  blocking collectives: 51.1 us -> 0 us
  starting transfers between devices: 23.4 us -> 0 us
  between operations: 14.2 us -> 0.79 us
    pallas_call x0 -> x2, Pallas kernels: none -> 200 us  [the longest x1 164 us: move(): pl.pallas_call(functools.partial(move_kernel, groups, count), out_shape=[...]
    all_to_all x2 -> x0, waiting for transfers between devices: 133 us -> none  [the longest x1 83.3 us: local(): lax.all_to_all(gate_train, 'expert', split_axis=0, concat_axis=1, tiled=T...]
    reduce_scatter x1 -> x0, waiting for transfers between devices: 68.5 us -> none  [local(): lax.psum_scatter(partial_out, 'expert', scatter_dimension=0, tiled=True)]
    all_to_all x1 -> x0, blocking collectives: 51.1 us -> none  [local(): lax.all_to_all(hidden_units, 'expert', split_axis=0, concat_axis=0, tiled...]
    all_to_all x2 -> x0, starting transfers between devices: 23.3 us -> none  [the longest x1 15.6 us: local(): lax.all_to_all(up_train, 'expert', split_axis=0, concat_axis=1, tiled=True)]
    dot_general x3 -> x2, matrix products: 21.5 us -> 21.5 us  [the longest x1 13.2 us: local(): jnp.dot(hidden_units, down_moved, preferred_element_type=jnp.float32)]
  transfers between devices with their start and end apart: 4 -> 0, of which waited for: 3 -> 0; matrix products, arithmetic and copies ran while one was open for 5% -> 0% of each run, Pallas kernels for 0% -> 0%
where the time goes in v2:
time: 233 us
  Pallas kernels  200 us (86%)
  matrix products  23.6 us (10%)
  other arithmetic  5.37 us (2%)
  local copies, waits for them, and re-layouts  3.25 us (1%)
    pallas_call x1, Pallas kernels, move(): pl.pallas_call(functools.partial(move_kernel, groups, count), out_shape=[...  164 us
    pallas_call x1, Pallas kernels, summed(): pl.pallas_call(functools.partial(sum_kernel, count), out_shape=jax.ShapeD...  35.9 us
    dot_general x1, matrix products, local(): jnp.dot(hidden_units, down_moved, preferred_element_type=jnp.float32)  13.2 us
    dot_general x1, matrix products, local(): up_proj = jnp.dot(tokens, up_moved, preferred_element_type=jnp.float32)  8.22 us

profile of v2, /device:TPU:0, one launch (start us, length us, event | category | flops | bytes accessed | tf_op | source)
XLA Modules:
  0.0 232.8 jit_solution(87257218601567009)
XLA Ops:
  0.6 0.0 copy-start
  0.6 0.7 convert_element_type.49
  1.4 1.1 fusion.11
  2.5 1.1 fusion.13
  3.6 0.7 fusion.21
  4.3 0.1 copy.31
  4.4 1.1 fusion.34
  5.6 0.2 fusion.26
  5.8 0.1 subtract_convert_fusion
  5.9 0.8 concatenate.3.rows_ref
  6.7 163.9 %shard_map.140 = (bf16[16,128,768]{2,1,0:T(8,128)(2,1)}, bf16[16,128,768]{2,1,0:T(8,128)(2,1)}, bf16[16,48,2048]{2,1,0:T(8,128)(2,1)}, bf16[16,64,2176]{2,1,0:T(8,128)(2,1)}) custom-call(bf16[16,128,768]{2,1,0:T(8,128)(2,1)} %gate_ref.1, bf16[16,128,768]{2,1,0:T(8,128)(2,1)} %up_ref.1, bf16[16,48,2048]{2,1,0:T(8,128)(2,1)} %down_ref.1, ...), custom_call_target="tpu_custom_call" | custom-call | tf_op jit(solution)/shard_map/pallas_call | solution.py:268
  170.5 8.2 %fusion = f32[1024,768]{1,0:T(8,128)} fusion(bf16[2048,768]{1,0:T(8,128)(2,1)} %bitcast.52, bf16[1024,2176]{1,0:T(8,128)(2,1)} %bitcast.47), kind=kOutput, calls=%fused_computation.1 | convolution fusion | flops 3221225472 | bytes 10485760 | tf_op jit(solution)/shard_map/dot_general | solution.py:471
  178.8 1.1 select_reduce_fusion
  179.9 13.2 %convolution_convert_fusion = bf16[1024,2048]{1,0:T(8,128)(2,1)} fusion(bf16[768,2048]{1,0:T(8,128)(2,1)} %bitcast.51, f32[1024,768]{1,0:T(8,128)} %fusion, bf16[2048,768]{1,0:T(8,128)(2,1)} %bitcast.50, bf16[1024,2176]{1,0:T(8,128)(2,1)} %bitcast.49, f32[1024]{0:T(1024)S(1)} %select_reduce_fusion), kind=kOutput, calls=%fused_computation | convolution fusion | flops 6450053120 | bytes 17829888 | tf_op jit(solution)/shard_map/dot_general | solution.py:473
  193.1 0.0 copy-start.5
  193.1 0.0 copy-start.1
  193.1 0.0 copy-start.2
  193.1 0.0 copy-start.4
  193.1 0.0 copy-start.3
  193.2 35.9 %shard_map.141 = bf16[64,2048]{1,0:T(8,128)(2,1)} custom-call(bf16[16,64,2048]{2,1,0:T(8,128)(2,1)} %bitcast.41), custom_call_target="tpu_custom_call" | custom-call | tf_op jit(solution)/shard_map/pallas_call | solution.py:421
  229.1 0.0 copy-done.5
  229.1 0.1 iota_compare_fusion.1
  229.2 0.0 copy-done.1
  229.2 0.0 copy-done.2
  229.2 0.5 fusion.33
  229.7 0.0 copy-done.4
  229.7 0.2 fusion.22
  229.8 0.2 fusion.18
  230.1 0.0 copy-done.3
  230.1 0.0 copy-done
  230.1 0.3 fusion.10
  230.5 0.7 copy.59
  231.1 1.7 copy.62
  (7 shorter events, 0.1 us)
Async XLA Ops:
  0.6 229.5 %copy-start = (bf16[8,64,512]{2,1,0:T(8,128)(2,1)S(1)}, bf16[8,64,512]{2,1,0:T(8,128)(2,1)}, u32[]{:S(2)}) copy-start(bf16[8,64,512]{2,1,0:T(8,128)(2,1)} %param.15) | copy-start | bytes 1572868
  193.1 36.0 %copy-start.5 = (s32[8]{0:T(128)S(1)}, s32[8]{0:T(128)}, u32[]{:S(2)}) copy-start(s32[8]{0:T(128)} %param.18) | copy-start | bytes 100
  193.1 36.1 %copy-start.1 = (bf16[8,64,512]{2,1,0:T(8,128)(2,1)S(1)}, bf16[8,64,512]{2,1,0:T(8,128)(2,1)}, u32[]{:S(2)}) copy-start(bf16[8,64,512]{2,1,0:T(8,128)(2,1)} %param.14) | copy-start | bytes 1572868
  193.1 36.1 %copy-start.2 = (bf16[8,4096]{1,0:T(8,128)(2,1)S(1)}, bf16[8,4096]{1,0:T(8,128)(2,1)}, u32[]{:S(2)}) copy-start(bf16[8,4096]{1,0:T(8,128)(2,1)} %param.13) | copy-start | bytes 196612
  193.1 36.5 %copy-start.4 = (bf16[8,512]{1,0:T(8,128)(2,1)S(1)}, bf16[8,512]{1,0:T(8,128)(2,1)}, u32[]{:S(2)}) copy-start(bf16[8,512]{1,0:T(8,128)(2,1)} %param.16) | copy-start | bytes 24580
  193.1 37.0 %copy-start.3 = (bf16[8,512]{1,0:T(8,128)(2,1)S(1)}, bf16[8,512]{1,0:T(8,128)(2,1)}, u32[]{:S(2)}) copy-start(bf16[8,512]{1,0:T(8,128)(2,1)} %param.17) | copy-start | bytes 24580

commit v3 on v2

--- a/solution.py
+++ b/solution.py
@@ -68,7 +68,8 @@
 
 
 MESH = pl.DeviceIdType.MESH
-AHEAD = 8
+AHEAD = 4
+NEAR = 4
 
 
 def greet(targets):
@@ -174,6 +175,11 @@
 
     def across(kind, r, refs_in, refs_out, which):
         target = me ^ r
+        if r < NEAR:
+            a, b = ((gate_ref, gate_out), (down_ref, down_out), (up_ref, up_out))[kind]
+            send = send_x.at[0, r, 0] if kind == 2 else send_w.at[kind, r]
+            recv = recv_x.at[0, r, 0] if kind == 2 else recv_w.at[kind, r]
+            return remote(a.at[target], b.at[me], send, recv, (group, target))
         if kind == 0:
             return remote(
                 refs_in[which].at[target, rows_of(group)], refs_out[which].at[me, rows_of(group)],
@@ -191,10 +197,10 @@
         pl.when(lax.rem(group, 2) == 1)(functools.partial(act, 1))
 
     def start_weight(kind, r):
-        if kind == 0:
+        if kind == 0 and r >= NEAR:
             by_matrix(lambda which: across(0, r, ins, outs, which).start())
         else:
-            across(1, r, ins, outs, 0).start()
+            across(kind, r, ins, outs, 0).start()
 
     def onward(kind, r, h, which):
         held = me ^ r
@@ -206,7 +212,7 @@
 
     def pass_on(kind, r):
         across(kind, r, ins, outs, 0).wait_recv()
-        for h in range(1, groups):
+        for h in range(1, groups if r >= NEAR else 1):
             if kind == 0:
                 by_matrix(lambda which: onward(0, r, h, which).start())
             else:
@@ -218,12 +224,14 @@
     ]
     half = count // 2
     order = [r for i in range(half) for r in ((half + i, i) if i else (half,))]
-    items = [(kind, r) for kind in range(2) for r in order]
-    side_at = 3 + 2 * (line - 1) + 2
+    first = [(kind, r) for r in order for kind in ((0, 2) if r < NEAR else (0,))]
+    items = first + [(1, r) for r in order]
+    spacing = len(items) // (line + 1)
+    side_at = 2 + spacing * (line - 1) + 3
     for i, item in enumerate(items):
         start_weight(*item)
-        if i >= 3 and (i - 3) % 2 == 0 and (i - 3) // 2 < line - 1:
-            line_step((i - 3) // 2)
+        if i >= 2 and (i - 2) % spacing == 0 and (i - 2) // spacing < line - 1:
+            line_step((i - 2) // spacing)
         if i == side_at:
             for index in range(line):
                 side_step(index)
@@ -243,7 +251,7 @@
         copy.wait()
     for kind, r in items:
         across(kind, r, ins, outs, 0).wait_send()
-        for h in range(1, groups):
+        for h in range(1, groups if r >= NEAR else 1):
             onward(kind, r, h, 0).wait()
     for index in range(line):
         block = lax.rem(me, 4) + 4 * index

time: 233 us -> 207 us (0.89)
  Pallas kernels: 200 us -> 173 us
    pallas_call x1, Pallas kernels: 164 us -> 137 us  [move(): pl.pallas_call(functools.partial(move_kernel, groups, count), out_shape=[...]
where the time goes in v3:
time: 207 us; the launch traced here: 206 us
  Pallas kernels  173 us (84%)
  matrix products  23.6 us (11%)
  other arithmetic  5.37 us (3%)
  local copies, waits for them, and re-layouts  3.25 us (2%)
    pallas_call x1, Pallas kernels, move(): pl.pallas_call(functools.partial(move_kernel, groups, count), out_shape=[...  137 us
    pallas_call x1, Pallas kernels, summed(): pl.pallas_call(functools.partial(sum_kernel, count), out_shape=jax.ShapeD...  36.7 us
    dot_general x1, matrix products, local(): jnp.dot(hidden_units, down_moved, preferred_element_type=jnp.float32)  13.2 us
    dot_general x1, matrix products, local(): up_proj = jnp.dot(tokens, up_moved, preferred_element_type=jnp.float32)  8.22 us

profile of v3, /device:TPU:0, one launch (start us, length us, event | category | flops | bytes accessed | tf_op | source)
XLA Modules:
  0.0 206.3 jit_solution(16430914229621846868)
XLA Ops:
  0.6 0.0 copy-start
  0.6 0.7 convert_element_type.49
  1.4 1.1 fusion.11
  2.5 1.1 fusion.13
  3.6 0.7 fusion.21
  4.3 0.1 copy.31
  4.4 1.1 fusion.34
  5.6 0.2 fusion.26
  5.8 0.1 subtract_convert_fusion
  5.9 0.8 concatenate.3.rows_ref
  6.7 136.7 %shard_map.140 = (bf16[16,128,768]{2,1,0:T(8,128)(2,1)}, bf16[16,128,768]{2,1,0:T(8,128)(2,1)}, bf16[16,48,2048]{2,1,0:T(8,128)(2,1)}, bf16[16,64,2176]{2,1,0:T(8,128)(2,1)}) custom-call(bf16[16,128,768]{2,1,0:T(8,128)(2,1)} %gate_ref.1, bf16[16,128,768]{2,1,0:T(8,128)(2,1)} %up_ref.1, bf16[16,48,2048]{2,1,0:T(8,128)(2,1)} %down_ref.1, ...), custom_call_target="tpu_custom_call" | custom-call | tf_op jit(solution)/shard_map/pallas_call | solution.py:276
  143.3 8.2 %fusion = f32[1024,768]{1,0:T(8,128)} fusion(bf16[2048,768]{1,0:T(8,128)(2,1)} %bitcast.52, bf16[1024,2176]{1,0:T(8,128)(2,1)} %bitcast.47), kind=kOutput, calls=%fused_computation.1 | convolution fusion | flops 3221225472 | bytes 10485760 | tf_op jit(solution)/shard_map/dot_general | solution.py:479
  151.6 1.1 select_reduce_fusion
  152.7 13.2 %convolution_convert_fusion = bf16[1024,2048]{1,0:T(8,128)(2,1)} fusion(bf16[768,2048]{1,0:T(8,128)(2,1)} %bitcast.51, f32[1024,768]{1,0:T(8,128)} %fusion, bf16[2048,768]{1,0:T(8,128)(2,1)} %bitcast.50, bf16[1024,2176]{1,0:T(8,128)(2,1)} %bitcast.49, f32[1024]{0:T(1024)S(1)} %select_reduce_fusion), kind=kOutput, calls=%fused_computation | convolution fusion | flops 6450053120 | bytes 17829888 | tf_op jit(solution)/shard_map/dot_general | solution.py:481
  165.9 0.0 copy-start.5
  165.9 0.0 copy-start.1
  165.9 0.0 copy-start.2
  165.9 0.0 copy-start.4
  165.9 0.0 copy-start.3
  165.9 36.7 %shard_map.141 = bf16[64,2048]{1,0:T(8,128)(2,1)} custom-call(bf16[16,64,2048]{2,1,0:T(8,128)(2,1)} %bitcast.41), custom_call_target="tpu_custom_call" | custom-call | tf_op jit(solution)/shard_map/pallas_call | solution.py:429
  202.6 0.0 copy-done.5
  202.6 0.1 iota_compare_fusion.1
  202.7 0.0 copy-done.1
  202.7 0.0 copy-done.2
  202.7 0.5 fusion.33
  203.2 0.0 copy-done.4
  203.2 0.2 fusion.22
  203.4 0.2 fusion.18
  203.6 0.0 copy-done.3
  203.7 0.0 copy-done
  203.7 0.3 fusion.10
  204.0 0.7 copy.59
  204.7 1.7 copy.62
  (7 shorter events, 0.1 us)
Async XLA Ops:
  0.6 203.0 %copy-start = (bf16[8,64,512]{2,1,0:T(8,128)(2,1)S(1)}, bf16[8,64,512]{2,1,0:T(8,128)(2,1)}, u32[]{:S(2)}) copy-start(bf16[8,64,512]{2,1,0:T(8,128)(2,1)} %param.15) | copy-start | bytes 1572868
  165.9 36.7 %copy-start.5 = (s32[8]{0:T(128)S(1)}, s32[8]{0:T(128)}, u32[]{:S(2)}) copy-start(s32[8]{0:T(128)} %param.18) | copy-start | bytes 100
  165.9 36.8 %copy-start.1 = (bf16[8,64,512]{2,1,0:T(8,128)(2,1)S(1)}, bf16[8,64,512]{2,1,0:T(8,128)(2,1)}, u32[]{:S(2)}) copy-start(bf16[8,64,512]{2,1,0:T(8,128)(2,1)} %param.14) | copy-start | bytes 1572868
  165.9 36.8 %copy-start.2 = (bf16[8,4096]{1,0:T(8,128)(2,1)S(1)}, bf16[8,4096]{1,0:T(8,128)(2,1)}, u32[]{:S(2)}) copy-start(bf16[8,4096]{1,0:T(8,128)(2,1)} %param.13) | copy-start | bytes 196612
  165.9 37.3 %copy-start.4 = (bf16[8,512]{1,0:T(8,128)(2,1)S(1)}, bf16[8,512]{1,0:T(8,128)(2,1)}, u32[]{:S(2)}) copy-start(bf16[8,512]{1,0:T(8,128)(2,1)} %param.16) | copy-start | bytes 24580
  165.9 37.7 %copy-start.3 = (bf16[8,512]{1,0:T(8,128)(2,1)S(1)}, bf16[8,512]{1,0:T(8,128)(2,1)}, u32[]{:S(2)}) copy-start(bf16[8,512]{1,0:T(8,128)(2,1)} %param.17) | copy-start | bytes 24580

commit v4 on v3

--- a/solution.py
+++ b/solution.py
@@ -92,7 +92,7 @@
 def move_kernel(
     groups, count,
     gate_ref, up_ref, down_ref, rows_ref,
-    gate_out, up_out, down_out, rows_out,
+    hidden_ref, down_out, gate_out, up_out, rows_out,
     send_w, recv_w, send_x, recv_x, local_sem, send_rows, recv_rows,
 ):
     me = lax.axis_index("expert")
@@ -222,12 +222,52 @@
         pltpu.make_async_copy(a.at[me], b.at[me], local_sem.at[i])
         for i, (a, b) in enumerate(((gate_ref, gate_out), (up_ref, up_out), (down_ref, down_out)))
     ]
+    width = gate_ref.shape[1] * count
+
+    def ready():
+        for index in range(line):
+            for y in range(2):
+                row_wait(4 * index + 2 * y + (lax.rem(me, 2) ^ 1))
+        own_rows.wait()
+        for copy in own_copies[:2]:
+            copy.wait()
+        for r in order:
+            for h in range(1, groups if r >= NEAR else 1):
+                onward(0, r, h, 0).wait_recv()
+
+    def expert_rows(quarter):
+        @pl.loop(0, count // 16)
+        def _(step):
+            at = quarter * (count // 4) + step * 4
+            rows = rows_out[pl.ds(at, 4)].reshape(-1, rows_out.shape[2])
+            tokens = rows[:, :width]
+            shares = rows[:, width:].astype(jnp.float32)
+            lane = lax.broadcasted_iota(jnp.int32, shares.shape, 1)
+            own = jnp.logical_or(lane == me, lane == me + count)
+            own_mix = jnp.sum(jnp.where(own, shares, 0.0), axis=1, keepdims=True)
+            gate = gate_out[...].reshape(width, -1)
+            gate_proj = jnp.dot(tokens, gate, preferred_element_type=jnp.float32)
+            up = up_out[...].reshape(width, -1)
+            up_proj = jnp.dot(tokens, up, preferred_element_type=jnp.float32)
+            hidden = gate_proj / (1.0 + jnp.exp(-gate_proj)) * up_proj * own_mix
+            place = pl.ds(pl.multiple_of(at * rows_out.shape[1], rows.shape[0]), rows.shape[0])
+            hidden_ref[place, :] = hidden.astype(hidden_ref.dtype)
+
     half = count // 2
     order = [r for i in range(half) for r in ((half + i, i) if i else (half,))]
     first = [(kind, r) for r in order for kind in ((0, 2) if r < NEAR else (0,))]
     items = first + [(1, r) for r in order]
     spacing = len(items) // (line + 1)
     side_at = 2 + spacing * (line - 1) + 3
+
+    def advance(i):
+        pass_on(*items[i])
+        before_last = len(items) - 1 - i
+        if before_last % 2 == 0 and before_last < 8:
+            if before_last == 6:
+                ready()
+            expert_rows(3 - before_last // 2)
+
     for i, item in enumerate(items):
         start_weight(*item)
         if i >= 2 and (i - 2) % spacing == 0 and (i - 2) // spacing < line - 1:
@@ -239,20 +279,17 @@
             for copy in own_copies:
                 copy.start()
         if i >= AHEAD:
-            pass_on(*items[i - AHEAD])
-    for item in items[len(items) - AHEAD :]:
-        pass_on(*item)
-
-    for index in range(line):
-        for y in range(2):
-            row_wait(4 * index + 2 * y + (lax.rem(me, 2) ^ 1))
-    own_rows.wait()
-    for copy in own_copies:
-        copy.wait()
+            advance(i - AHEAD)
+    for i in range(len(items) - AHEAD, len(items)):
+        advance(i)
+
+    own_copies[2].wait()
     for kind, r in items:
         across(kind, r, ins, outs, 0).wait_send()
         for h in range(1, groups if r >= NEAR else 1):
-            onward(kind, r, h, 0).wait()
+            onward(kind, r, h, 0).wait_send()
+            if kind == 1:
+                onward(kind, r, h, 0).wait_recv()
     for index in range(line):
         block = lax.rem(me, 4) + 4 * index
 
@@ -276,19 +313,20 @@
     return pl.pallas_call(
         functools.partial(move_kernel, groups, count),
         out_shape=[
-            jax.ShapeDtypeStruct(gate_train.shape, gate_train.dtype),
-            jax.ShapeDtypeStruct(up_train.shape, up_train.dtype),
+            jax.ShapeDtypeStruct((count * row_block.shape[0], gate_train.shape[2]), jnp.bfloat16),
             jax.ShapeDtypeStruct(down_train.shape, down_train.dtype),
-            jax.ShapeDtypeStruct((count,) + row_block.shape, row_block.dtype),
         ],
         in_specs=[anywhere, anywhere, anywhere, pl.BlockSpec(memory_space=pltpu.VMEM)],
-        out_specs=[anywhere] * 4,
+        out_specs=[pl.BlockSpec(memory_space=pltpu.VMEM), anywhere],
         scratch_shapes=[
+            pltpu.VMEM(gate_train.shape, gate_train.dtype),
+            pltpu.VMEM(up_train.shape, up_train.dtype),
+            pltpu.VMEM((count,) + row_block.shape, row_block.dtype),
             DMA((2, count)), DMA((2, count)),
             DMA((2, count, max(1, groups - 1))), DMA((2, count, max(1, groups - 1))),
             DMA((4,)), DMA((4, count)), DMA((count,)),
         ],
-        compiler_params=pltpu.CompilerParams(collective_id=0, has_side_effects=True),
+        compiler_params=pltpu.CompilerParams(collective_id=0, has_side_effects=True, vmem_limit_bytes=60 * 2**20),
     )(gate_train, up_train, down_train, row_block)
 
 
@@ -462,22 +500,11 @@
     row_block = jnp.concatenate(
         [normed, mixing_high, mixing_low, jnp.zeros((normed.shape[0], spare), jnp.bfloat16)], axis=1
     )
-    gate_moved, up_moved, down_moved, all_rows = move(
+    hidden_units, down_moved = move(
         lax.axis_size("groups"), gate_train, up_train, down_train, row_block
     )
-    all_rows = all_rows.reshape(-1, all_rows.shape[-1])
-    gate_moved = gate_moved.reshape(-1, gate_moved.shape[-1])
-    up_moved = up_moved.reshape(-1, up_moved.shape[-1])
     down_moved = down_moved.reshape(-1, width)
     attended = attend(queries, key_cache, value_cache, new_key, new_value, cache_lengths)
-    own_index = lax.axis_index("expert")
-    tokens = all_rows[:, :width]
-    mix_parts = all_rows[:, width : width + 2 * expert_count].astype(jnp.float32)
-    own_column = jnp.arange(2 * expert_count) % expert_count == own_index
-    own_mix = jnp.sum(jnp.where(own_column[None, :], mix_parts, 0.0), axis=1)
-    gate_proj = jnp.dot(tokens, gate_moved, preferred_element_type=jnp.float32)
-    up_proj = jnp.dot(tokens, up_moved, preferred_element_type=jnp.float32)
-    hidden_units = (jax.nn.silu(gate_proj) * up_proj * own_mix[:, None]).astype(jnp.bfloat16)
     partial_out = jnp.dot(hidden_units, down_moved, preferred_element_type=jnp.float32).astype(jnp.bfloat16)
     mixed_out = summed(partial_out, expert_count)
     return (attended, mixed_out)

time: 207 us -> 193 us (0.932)
  matrix products: 23.6 us -> 9.81 us
    dot_general x1 -> x0, matrix products: 8.22 us -> none  [local(): up_proj = jnp.dot(tokens, up_moved, preferred_element_type=jnp.float32)]
    dot_general x1, matrix products: 13.2 us -> 7.71 us  [local(): jnp.dot(hidden_units, down_moved, preferred_element_type=jnp.float32)]
where the time goes in v4:
time: 193 us; the launch traced here: 192 us
  Pallas kernels  174 us (90%)
  matrix products  9.81 us (5%)
  other arithmetic  4.27 us (2%)
  local copies, waits for them, and re-layouts  3.27 us (2%)
    pallas_call x1, Pallas kernels, move(): pl.pallas_call(functools.partial(move_kernel, groups, count), out_shape=[...  137 us
    pallas_call x1, Pallas kernels, summed(): pl.pallas_call(functools.partial(sum_kernel, count), out_shape=jax.ShapeD...  37.3 us
    dot_general x1, matrix products, local(): jnp.dot(hidden_units, down_moved, preferred_element_type=jnp.float32)  7.71 us

profile of v4, /device:TPU:0, one launch (start us, length us, event | category | flops | bytes accessed | tf_op | source)
XLA Modules:
  0.0 192.4 jit_solution(14041173040760905776)
XLA Ops:
  0.6 0.0 copy-start
  0.6 0.7 convert_element_type.43
  1.4 1.1 fusion.3
  2.5 1.1 fusion.5
  3.6 0.7 fusion.13
  4.3 0.1 copy.31
  4.4 1.1 fusion.24
  5.6 0.2 fusion.18
  5.8 0.1 subtract_convert_fusion
  5.9 0.8 concatenate.3.rows_ref
  6.7 137.0 %shard_map.140 = (bf16[1024,768]{1,0:T(8,128)(2,1)}, bf16[16,48,2048]{2,1,0:T(8,128)(2,1)}) custom-call(bf16[16,128,768]{2,1,0:T(8,128)(2,1)} %gate_ref.1, bf16[16,128,768]{2,1,0:T(8,128)(2,1)} %up_ref.1, bf16[16,48,2048]{2,1,0:T(8,128)(2,1)} %down_ref.1, bf16[64,2176]{1,0:T(8,128)(2,1)} %concatenate.3.rows_ref), custom_call_target="tpu_custom_call" | custom-call | tf_op jit(solution)/shard_map/pallas_call | solution.py:313
  143.7 7.7 %convolution_convert_fusion = bf16[1024,2048]{1,0:T(8,128)(2,1)} fusion(bf16[1024,768]{1,0:T(8,128)(2,1)} %get-tuple-element.4, bf16[768,2048]{1,0:T(8,128)(2,1)} %bitcast.43), kind=kOutput, calls=%fused_computation | convolution fusion | flops 3223322624 | bytes 8912896 | tf_op jit(solution)/shard_map/dot_general | solution.py:508
  151.4 0.0 copy-start.5
  151.4 0.0 copy-start.1
  151.4 0.0 copy-start.2
  151.4 0.0 copy-start.4
  151.4 0.0 copy-start.3
  151.4 37.3 %shard_map.141 = bf16[64,2048]{1,0:T(8,128)(2,1)} custom-call(bf16[16,64,2048]{2,1,0:T(8,128)(2,1)} %bitcast.37), custom_call_target="tpu_custom_call" | custom-call | tf_op jit(solution)/shard_map/pallas_call | solution.py:467
  188.7 0.0 copy-done.5
  188.7 0.1 iota_compare_fusion.1
  188.8 0.0 copy-done.1
  188.8 0.0 copy-done.2
  188.8 0.5 fusion.23
  189.3 0.0 copy-done.4
  189.3 0.2 fusion.14
  189.5 0.2 fusion.10
  189.7 0.0 copy-done.3
  189.8 0.0 copy-done
  189.8 0.3 fusion.2
  190.1 0.7 copy.59
  190.8 1.7 copy.62
  (6 shorter events, 0.1 us)
Async XLA Ops:
  0.6 189.1 %copy-start = (bf16[8,64,512]{2,1,0:T(8,128)(2,1)S(1)}, bf16[8,64,512]{2,1,0:T(8,128)(2,1)}, u32[]{:S(2)}) copy-start(bf16[8,64,512]{2,1,0:T(8,128)(2,1)} %param.15) | copy-start | bytes 1572868
  151.4 37.4 %copy-start.5 = (s32[8]{0:T(128)S(1)}, s32[8]{0:T(128)}, u32[]{:S(2)}) copy-start(s32[8]{0:T(128)} %param.18) | copy-start | bytes 100
  151.4 37.4 %copy-start.1 = (bf16[8,64,512]{2,1,0:T(8,128)(2,1)S(1)}, bf16[8,64,512]{2,1,0:T(8,128)(2,1)}, u32[]{:S(2)}) copy-start(bf16[8,64,512]{2,1,0:T(8,128)(2,1)} %param.14) | copy-start | bytes 1572868
  151.4 37.4 %copy-start.2 = (bf16[8,4096]{1,0:T(8,128)(2,1)S(1)}, bf16[8,4096]{1,0:T(8,128)(2,1)}, u32[]{:S(2)}) copy-start(bf16[8,4096]{1,0:T(8,128)(2,1)} %param.13) | copy-start | bytes 196612
  151.4 37.9 %copy-start.4 = (bf16[8,512]{1,0:T(8,128)(2,1)S(1)}, bf16[8,512]{1,0:T(8,128)(2,1)}, u32[]{:S(2)}) copy-start(bf16[8,512]{1,0:T(8,128)(2,1)} %param.16) | copy-start | bytes 24580
  151.4 38.3 %copy-start.3 = (bf16[8,512]{1,0:T(8,128)(2,1)S(1)}, bf16[8,512]{1,0:T(8,128)(2,1)}, u32[]{:S(2)}) copy-start(bf16[8,512]{1,0:T(8,128)(2,1)} %param.17) | copy-start | bytes 24580
